TPU v7x, 256 devices: a whole 4x4x8 slice. The times are simulated.
256 devices in a mesh: freq: 8 (over x_lo, y), src: 32 (over x_hi, z, core).
Axes of the slice: x: 4 (x_hi: 2, x_lo: 2; x = x_hi * 2 + x_lo), y: 4, z: 8, core: 2. Of those that a mesh axis runs over, the one named last changes fastest.
Arguments:
- recorded: float32 [4096, 512, 128], P('src', 'freq'), may hold values from -0.54 to 0.54
- panels: float32 [512, 512, 128], P('src', 'freq'), may hold values from -0.18 to 0.18
Outputs:
- multiples: float32 [4096, 512, 128], P('src', 'freq')
All inputs are finite; a program needn't handle non-finite values.
Results may differ from a plain program's by a relative error of at most 0.00007.
Values sent between devices are 32-bit elements; how exact they have to be, the bound alone decides.
A program may use at most 128 MiB of HBM per device.

v0:
```python
import functools

import jax
import jax.numpy as jnp
import numpy as np
from jax import lax
from jax.experimental import pallas as pl
from jax.experimental.pallas import tpu as pltpu
from jax.sharding import PartitionSpec as P

NT = 128
NF = 64
SLOTS = 4
MESH = pl.DeviceIdType.MESH
F32 = jnp.float32
BF16 = jnp.bfloat16

PLANE = [
    (1, 0), (0, 1), (3, 0), (0, 3), (1, 2), (2, 1), (3, 2), (2, 3),
    (1, 1), (3, 3), (2, 2), (1, 3), (3, 1), (2, 0), (0, 2),
]


def lookup_tables():
    phase = np.arange(NF)[:, None] * np.arange(NT)[None, :] % NT
    angle = 2.0 * np.pi / NT * phase
    forward = np.stack([np.cos(angle), -np.sin(angle)], axis=1)
    weight = np.where(np.arange(NF) == 0, 1.0, 2.0) / NT
    inverse = forward * weight[:, None, None]
    shape = (2 * NF, NT)
    return forward.reshape(shape).astype(np.float32), inverse.reshape(shape).astype(np.float32)


def split(value):
    high = value.astype(BF16)
    return high, (value - high.astype(F32)).astype(BF16)


def halves(first, second):
    lane = lax.broadcasted_iota(jnp.int32, first.shape, first.ndim - 1)
    low = jnp.where(lane < 64, first, pltpu.roll(second, 64, axis=first.ndim - 1))
    high = jnp.where(lane < 64, pltpu.roll(first, 64, axis=first.ndim - 1), second)
    return low, high


def kernel(
    rec_hbm, pan_hbm, fwd_ref, inv_ref, out_hbm,
    x_buf, p_buf, g_send, g_recv, g_all, d_send, d_recv, d_hi, d_lo, g_hi, g_lo, m_send, m_recv, o_buf,
    x_sem, p_sem, o_sem, gs_sem, gr_sem, ds_sem, dr_sem, ms_sem, mr_sem,
    fs_sem, fr_sem, bs_sem, br_sem, cs_sem, cr_sem,
):
    own_o = lax.axis_index("freq")
    src = lax.axis_index("src")
    own_xhi = src // 16
    zc = lax.rem(src, 16)
    z = zc // 2
    core = lax.rem(zc, 2)
    x = own_xhi * 2 + own_o // 4
    y = lax.rem(own_o, 4)
    own_q = own_xhi * 8 + own_o

    def plane(offset):
        px = lax.rem(x + offset[0], 4)
        py = lax.rem(y + offset[1], 4)
        o = lax.rem(px, 2) * 4 + py
        return o, px // 2

    def plane_id(offset):
        o, xhi = plane(offset)
        return (o, xhi * 16 + zc)

    step = 1 - 2 * core
    z_ahead = lax.rem(z + step + 8, 8)
    z_behind = lax.rem(z - step + 8, 8)
    ahead_id = (own_o, own_xhi * 16 + z_ahead * 2 + core)
    behind_id = (own_o, own_xhi * 16 + z_behind * 2 + core)
    partner_id = (own_o, own_xhi * 16 + z * 2 + 1 - core)

    pan_copy = pltpu.make_async_copy(pan_hbm, p_buf, p_sem)
    pan_copy.start()

    def rec_copy(chunk, half):
        rows = pl.ds(half * 64 + chunk * 16, 16)
        return pltpu.make_async_copy(rec_hbm.at[rows], x_buf.at[rows], x_sem.at[chunk, half])

    for chunk in range(4):
        for half in range(2):
            rec_copy(chunk, half).start()

    barrier = pltpu.get_barrier_semaphore()
    others = [plane_id(offset) for offset in PLANE] + [ahead_id, behind_id, partner_id]
    for other in others:
        pl.semaphore_signal(barrier, inc=1, device_id=other, device_id_type=MESH)

    nt = (((1,), (1,)), ((), ()))
    tn = (((0,), (0,)), ((), ()))

    pan_copy.wait()
    for kp in range(0, 8, 2):
        rows = jnp.concatenate([p_buf[kp], p_buf[kp + 8], p_buf[kp + 1], p_buf[kp + 9]], axis=0)
        hat = lax.dot_general(fwd_ref[...], rows, nt, precision=lax.Precision.HIGH, preferred_element_type=F32)
        g_send[pl.ds(kp, 128, stride=8), :] = hat[:, :128]
        g_send[pl.ds(kp + 1, 128, stride=8), :] = hat[:, 128:]

    pl.semaphore_wait(barrier, len(others))

    def g_copy(n):
        o, xhi = plane(PLANE[n])
        return pltpu.make_async_remote_copy(
            src_ref=g_send.at[pl.ds((xhi * 8 + o) * 64, 64)],
            dst_ref=g_recv.at[own_q],
            send_sem=gs_sem.at[n], recv_sem=gr_sem.at[n],
            device_id=plane_id(PLANE[n]), device_id_type=MESH,
        )

    for n in range(15):
        g_copy(n).start()
    g_recv[own_q] = g_send[pl.ds(own_q * 64, 64), :]

    for chunk in range(4):
        for half in range(2):
            rec_copy(chunk, half).wait()

        @pl.loop(0, 8)
        def _(pair):
            ih = chunk * 16 + pair * 2
            rows = jnp.concatenate([x_buf[ih], x_buf[ih + 64], x_buf[ih + 1], x_buf[ih + 65]], axis=0)
            hat = lax.dot_general(fwd_ref[...], rows, nt, precision=lax.Precision.HIGH, preferred_element_type=F32)
            d_send[pl.ds(ih, 128, stride=64), :] = hat[:, :128]
            d_send[pl.ds(ih + 1, 128, stride=64), :] = hat[:, 128:]

    def d_copy(slot, n):
        o, xhi = plane(PLANE[n])
        return pltpu.make_async_remote_copy(
            src_ref=d_send.at[pl.ds(((xhi * 8 + o) * SLOTS + slot) * 128, 128)],
            dst_ref=d_recv.at[slot, own_q],
            send_sem=ds_sem.at[slot, n], recv_sem=dr_sem.at[slot, n],
            device_id=plane_id(PLANE[n]), device_id_type=MESH,
        )

    @pl.loop(0, SLOTS)
    def _(slot):
        for n in range(15):
            d_copy(slot, n).start()

    @pl.loop(0, SLOTS)
    def _(slot):
        d_recv[slot, own_q] = d_send[pl.ds((own_q * SLOTS + slot) * 128, 128), :]

    for n in range(15):
        g_copy(n).wait_recv()

    @pl.loop(0, SLOTS)
    def _(slot):
        for c in range(2):
            rows = pl.ds((slot * 2 + c) * 8, 8)
            for xhi in range(2):
                for pair in range(4):
                    low, high = halves(g_recv[xhi * 8 + 2 * pair, rows, :], g_recv[xhi * 8 + 2 * pair + 1, rows, :])
                    g_all[slot, zc, c, xhi, 0:8, pair * 128:(pair + 1) * 128] = low
                    g_all[slot, zc, c, xhi, 8:16, pair * 128:(pair + 1) * 128] = high

    def block(hop, way):
        return lax.rem(z - way * hop * step + 32, 8) * 2 + core

    def ahead_copy(slot, hop):
        ref = g_all.at[slot, block(hop, 1)]
        return pltpu.make_async_remote_copy(
            src_ref=ref, dst_ref=ref, send_sem=fs_sem.at[slot, hop], recv_sem=fr_sem.at[slot, hop],
            device_id=ahead_id, device_id_type=MESH,
        )

    def behind_copy(slot, hop):
        ref = g_all.at[slot, block(hop, -1)]
        return pltpu.make_async_remote_copy(
            src_ref=ref, dst_ref=ref, send_sem=bs_sem.at[slot, hop], recv_sem=br_sem.at[slot, hop],
            device_id=behind_id, device_id_type=MESH,
        )

    def partner_copy(slot, n):
        ref = g_all.at[slot, block(n, 1) if n < 5 else block(n - 4, -1)]
        return pltpu.make_async_remote_copy(
            src_ref=ref, dst_ref=ref, send_sem=cs_sem.at[slot, n], recv_sem=cr_sem.at[slot, n],
            device_id=partner_id, device_id_type=MESH,
        )

    @pl.loop(0, SLOTS)
    def _(slot):
        ahead_copy(slot, 0).start()
        behind_copy(slot, 0).start()
        partner_copy(slot, 0).start()

    for hop in range(4):
        @pl.loop(0, SLOTS)
        def _(slot):
            ahead_copy(slot, hop).wait_recv()
            if hop < 3:
                ahead_copy(slot, hop + 1).start()
            partner_copy(slot, hop + 1).start()
            if hop < 3:
                behind_copy(slot, hop).wait_recv()
                if hop < 2:
                    behind_copy(slot, hop + 1).start()
                partner_copy(slot, hop + 5).start()

    def m_copy(slot, n):
        o, xhi = plane(PLANE[n])
        return pltpu.make_async_remote_copy(
            src_ref=m_send.at[slot, xhi * 8 + o],
            dst_ref=m_recv.at[pl.ds((own_q * SLOTS + slot) * 128, 128)],
            send_sem=ms_sem.at[slot, n], recv_sem=mr_sem.at[slot, n],
            device_id=plane_id(PLANE[n]), device_id_type=MESH,
        )

    def dot(left, right):
        return jnp.dot(left, right, preferred_element_type=F32)

    @pl.loop(0, SLOTS)
    def _(slot):
        for n in range(8):
            partner_copy(slot, n).wait_recv()

        @pl.loop(0, 16)
        def _(b):
            for c in range(2):
                for xhi in range(2):
                    high, low = split(g_all[slot, b, c, xhi])
                    rows = pl.ds(xhi * 256 + b * 16, 16)
                    g_hi[c, rows, :] = high
                    g_lo[c, rows, :] = low

        for n in range(15):
            d_copy(slot, n).wait_recv()

        for xhi in range(2):
            for pair in range(4):
                for c in range(2):
                    rows = pl.ds(c * 64, 64)
                    top, bottom = halves(
                        d_recv[slot, xhi * 8 + 2 * pair, rows, :], d_recv[slot, xhi * 8 + 2 * pair + 1, rows, :]
                    )
                    for at, part in ((0, top), (64, bottom)):
                        high, low = split(part)
                        d_hi[c, xhi * 128 + at:xhi * 128 + at + 64, pair * 128:(pair + 1) * 128] = high
                        d_lo[c, xhi * 128 + at:xhi * 128 + at + 64, pair * 128:(pair + 1) * 128] = low

        @pl.loop(0, 2)
        def _(xhi):
            rows = pl.ds(xhi * 128, 128)
            for tile in range(2):
                cols = slice(tile * 256, (tile + 1) * 256)

                def product(a, b):
                    return (
                        dot(d_hi[a, rows, :], g_hi[b, :, cols])
                        + dot(d_hi[a, rows, :], g_lo[b, :, cols])
                        + dot(d_lo[a, rows, :], g_hi[b, :, cols])
                    )

                real = product(0, 0) - product(1, 1)
                imag = product(0, 1) + product(1, 0)
                for c, value in ((0, real), (1, imag)):
                    for lanes in range(2):
                        part = value[:, lanes * 128:(lanes + 1) * 128]
                        even, odd = halves(part[:64], part[64:])
                        o = tile * 4 + lanes * 2
                        m_send[slot, xhi * 8 + o, c * 64:(c + 1) * 64, :] = even
                        m_send[slot, xhi * 8 + o + 1, c * 64:(c + 1) * 64, :] = odd

        for n in range(15):
            m_copy(slot, n).start()
        m_recv[pl.ds((own_q * SLOTS + slot) * 128, 128), :] = m_send[slot, own_q]

    @pl.loop(0, SLOTS)
    def _(slot):
        for n in range(15):
            m_copy(slot, n).wait_recv()

    def out_copy(chunk, half):
        rows = pl.ds(half * 64 + chunk * 16, 16)
        return pltpu.make_async_copy(o_buf.at[rows], out_hbm.at[rows], o_sem.at[chunk, half])

    for chunk in range(4):
        @pl.loop(0, 8)
        def _(pair):
            for u in range(2):
                ih = chunk * 16 + pair * 2 + u
                part = m_recv[pl.ds(ih, 128, stride=64), :]
                value = lax.dot_general(part, inv_ref[...], tn, precision=lax.Precision.HIGH, preferred_element_type=F32)
                o_buf[ih] = value[:64]
                o_buf[ih + 64] = value[64:]

        for half in range(2):
            out_copy(chunk, half).start()

    for n in range(15):
        g_copy(n).wait_send()

    @pl.loop(0, SLOTS)
    def _(slot):
        for n in range(15):
            d_copy(slot, n).wait_send()
            m_copy(slot, n).wait_send()
        for hop in range(4):
            ahead_copy(slot, hop).wait_send()
        for hop in range(3):
            behind_copy(slot, hop).wait_send()
        for n in range(8):
            partner_copy(slot, n).wait_send()

    for chunk in range(4):
        for half in range(2):
            out_copy(chunk, half).wait()


def local(recorded, panels):
    forward, inverse = lookup_tables()
    dma = pltpu.SemaphoreType.DMA
    return pl.pallas_call(
        kernel,
        out_shape=jax.ShapeDtypeStruct((128, 64, NT), F32),
        in_specs=[
            pl.BlockSpec(memory_space=pl.ANY),
            pl.BlockSpec(memory_space=pl.ANY),
            pl.BlockSpec(memory_space=pltpu.VMEM),
            pl.BlockSpec(memory_space=pltpu.VMEM),
        ],
        out_specs=pl.BlockSpec(memory_space=pl.ANY),
        scratch_shapes=[
            pltpu.VMEM((128, 64, NT), F32),
            pltpu.VMEM((16, 64, NT), F32),
            pltpu.VMEM((1024, 128), F32),
            pltpu.VMEM((16, 64, 128), F32),
            pltpu.VMEM((SLOTS, 16, 2, 2, 16, 512), F32),
            pltpu.VMEM((8192, 128), F32),
            pltpu.VMEM((SLOTS, 16, 128, 128), F32),
            pltpu.VMEM((2, 256, 512), BF16),
            pltpu.VMEM((2, 256, 512), BF16),
            pltpu.VMEM((2, 512, 512), BF16),
            pltpu.VMEM((2, 512, 512), BF16),
            pltpu.VMEM((SLOTS, 16, 128, 128), F32),
            pltpu.VMEM((8192, 128), F32),
            pltpu.VMEM((128, 64, NT), F32),
            dma((4, 2)), dma, dma((4, 2)),
            dma((15,)), dma((15,)),
            dma((SLOTS, 15)), dma((SLOTS, 15)),
            dma((SLOTS, 15)), dma((SLOTS, 15)),
            dma((SLOTS, 4)), dma((SLOTS, 4)),
            dma((SLOTS, 3)), dma((SLOTS, 3)),
            dma((SLOTS, 8)), dma((SLOTS, 8)),
        ],
        compiler_params=pltpu.CompilerParams(
            collective_id=0, has_side_effects=True, vmem_limit_bytes=56 * 1024 * 1024
        ),
        name="convolve",
    )(recorded, panels, jnp.asarray(forward), jnp.asarray(inverse))


def solution(mesh):
    return jax.shard_map(
        local,
        mesh=mesh,
        in_specs=(P("src", "freq", None), P("src", "freq", None)),
        out_specs=P("src", "freq", None),
        check_vma=False,
    )
```

profile of v0, /device:TPU:145, one launch (start us, length us, event | category | flops | bytes accessed | tf_op | source)
XLA Modules:
  0.0 131.8 jit_solution(4656359760559162923)
XLA Ops:
  0.0 127.0 %convolve.1 = f32[128,64,128]{2,1,0:T(8,128)} custom-call(f32[128,64,128]{2,1,0:T(8,128)} %rec_hbm.1, f32[16,64,128]{2,1,0:T(8,128)} %pan_hbm.1, f32[128,128]{1,0:T(8,128)} %constant.4.clone.fwd_ref, f32[128,128]{1,0:T(8,128)} %constant.5.clone.inv_ref), custom_call_target="tpu_custom_call" | custom-call | tf_op jit(solution)/shard_map/convolve/pallas_call | solution.py:319
  127.0 4.8 %copy.6 = f32[128,64,128]{2,1,0:T(8,128)} copy(f32[128,64,128]{2,1,0:T(8,128)} %convolve.1) | data formatting | bytes 8388608
where the time goes:
time: 132 us
  Pallas kernels  127 us (96%)
  local copies, waits for them, and re-layouts  4.79 us (4%)
    pallas_call x1, Pallas kernels, local(): pl.pallas_call(kernel, out_shape=jax.ShapeDtypeStruct((128, 64, NT), F32)...  127 us
    unnamed x1, local copies, waits for them, and re-layouts  4.79 us

commit v1 on v0

--- a/solution.py
+++ b/solution.py
@@ -27,8 +27,15 @@
     forward = np.stack([np.cos(angle), -np.sin(angle)], axis=1)
     weight = np.where(np.arange(NF) == 0, 1.0, 2.0) / NT
     inverse = forward * weight[:, None, None]
-    shape = (2 * NF, NT)
-    return forward.reshape(shape).astype(np.float32), inverse.reshape(shape).astype(np.float32)
+    forward = forward.reshape(2 * NF, NT)
+    inverse = inverse.reshape(16, SLOTS, 2, NT).transpose(1, 0, 2, 3).reshape(2 * NF, NT)
+    return [np.asarray(part) for table in (forward, inverse) for part in split_table(table)]
+
+
+def split_table(table):
+    high = table.astype(np.float32).astype(BF16)
+    low = (table - high.astype(np.float64)).astype(np.float32).astype(BF16)
+    return high, low
 
 
 def split(value):
@@ -44,9 +51,9 @@
 
 
 def kernel(
-    rec_hbm, pan_hbm, fwd_ref, inv_ref, out_hbm,
-    x_buf, p_buf, g_send, g_recv, g_all, d_send, d_recv, d_hi, d_lo, g_hi, g_lo, m_send, m_recv, o_buf,
-    x_sem, p_sem, o_sem, gs_sem, gr_sem, ds_sem, dr_sem, ms_sem, mr_sem,
+    rec_hbm, pan_hbm, fwd_hi, fwd_lo, inv_hi, inv_lo, acc_ref, m_last,
+    x_buf, p_buf, g_send, g_recv, g_all, d_send, d_recv, d_hi, d_lo, g_hi, g_lo, m_send, m_recv,
+    x_sem, p_sem, gs_sem, gr_sem, ds_sem, dr_sem, ms_sem, mr_sem,
     fs_sem, fr_sem, bs_sem, br_sem, cs_sem, cr_sem,
 ):
     own_o = lax.axis_index("freq")
@@ -93,12 +100,19 @@
         pl.semaphore_signal(barrier, inc=1, device_id=other, device_id_type=MESH)
 
     nt = (((1,), (1,)), ((), ()))
-    tn = (((0,), (0,)), ((), ()))
+
+    def forward(rows):
+        high, low = split(rows)
+        return (
+            lax.dot_general(fwd_hi[...], high, nt, preferred_element_type=F32)
+            + lax.dot_general(fwd_hi[...], low, nt, preferred_element_type=F32)
+            + lax.dot_general(fwd_lo[...], high, nt, preferred_element_type=F32)
+        )
 
     pan_copy.wait()
     for kp in range(0, 8, 2):
         rows = jnp.concatenate([p_buf[kp], p_buf[kp + 8], p_buf[kp + 1], p_buf[kp + 9]], axis=0)
-        hat = lax.dot_general(fwd_ref[...], rows, nt, precision=lax.Precision.HIGH, preferred_element_type=F32)
+        hat = forward(rows)
         g_send[pl.ds(kp, 128, stride=8), :] = hat[:, :128]
         g_send[pl.ds(kp + 1, 128, stride=8), :] = hat[:, 128:]
 
@@ -125,7 +139,7 @@
         def _(pair):
             ih = chunk * 16 + pair * 2
             rows = jnp.concatenate([x_buf[ih], x_buf[ih + 64], x_buf[ih + 1], x_buf[ih + 65]], axis=0)
-            hat = lax.dot_general(fwd_ref[...], rows, nt, precision=lax.Precision.HIGH, preferred_element_type=F32)
+            hat = forward(rows)
             d_send[pl.ds(ih, 128, stride=64), :] = hat[:, :128]
             d_send[pl.ds(ih + 1, 128, stride=64), :] = hat[:, 128:]
 
@@ -205,9 +219,13 @@
 
     def m_copy(slot, n):
         o, xhi = plane(PLANE[n])
+        if slot is None:
+            slot, dst = SLOTS - 1, m_last
+        else:
+            dst = m_recv.at[slot]
         return pltpu.make_async_remote_copy(
             src_ref=m_send.at[slot, xhi * 8 + o],
-            dst_ref=m_recv.at[pl.ds((own_q * SLOTS + slot) * 128, 128)],
+            dst_ref=dst.at[pl.ds(own_q * 128, 128)],
             send_sem=ms_sem.at[slot, n], recv_sem=mr_sem.at[slot, n],
             device_id=plane_id(PLANE[n]), device_id_type=MESH,
         )
@@ -215,8 +233,7 @@
     def dot(left, right):
         return jnp.dot(left, right, preferred_element_type=F32)
 
-    @pl.loop(0, SLOTS)
-    def _(slot):
+    def predict(slot):
         for n in range(8):
             partner_copy(slot, n).wait_recv()
 
@@ -267,40 +284,43 @@
                         m_send[slot, xhi * 8 + o, c * 64:(c + 1) * 64, :] = even
                         m_send[slot, xhi * 8 + o + 1, c * 64:(c + 1) * 64, :] = odd
 
+    @pl.loop(0, SLOTS - 1)
+    def _(slot):
+        predict(slot)
         for n in range(15):
             m_copy(slot, n).start()
-        m_recv[pl.ds((own_q * SLOTS + slot) * 128, 128), :] = m_send[slot, own_q]
+        m_recv[slot, pl.ds(own_q * 128, 128), :] = m_send[slot, own_q]
+
+    predict(SLOTS - 1)
+    for n in range(15):
+        m_copy(None, n).start()
+    m_last[pl.ds(own_q * 128, 128), :] = m_send[SLOTS - 1, own_q]
+
+    @pl.loop(0, SLOTS - 1)
+    def _(slot):
+        for n in range(15):
+            m_copy(slot, n).wait_recv()
+
+    @pl.loop(0, 32)
+    def _(pair):
+        for u in range(2):
+            ih = pair * 2 + u
+            part = jnp.concatenate([m_recv[slot, pl.ds(ih, 32, stride=64), :] for slot in range(SLOTS - 1)], axis=0)
+            high, low = split(part.T)
+            value = dot(high, inv_hi[0:96]) + dot(low, inv_hi[0:96]) + dot(high, inv_lo[0:96])
+            acc_ref[ih] = value[:64]
+            acc_ref[ih + 64] = value[64:]
+
+    for n in range(15):
+        m_copy(None, n).wait_recv()
+
+    for n in range(15):
+        g_copy(n).wait_send()
 
     @pl.loop(0, SLOTS)
     def _(slot):
         for n in range(15):
-            m_copy(slot, n).wait_recv()
-
-    def out_copy(chunk, half):
-        rows = pl.ds(half * 64 + chunk * 16, 16)
-        return pltpu.make_async_copy(o_buf.at[rows], out_hbm.at[rows], o_sem.at[chunk, half])
-
-    for chunk in range(4):
-        @pl.loop(0, 8)
-        def _(pair):
-            for u in range(2):
-                ih = chunk * 16 + pair * 2 + u
-                part = m_recv[pl.ds(ih, 128, stride=64), :]
-                value = lax.dot_general(part, inv_ref[...], tn, precision=lax.Precision.HIGH, preferred_element_type=F32)
-                o_buf[ih] = value[:64]
-                o_buf[ih + 64] = value[64:]
-
-        for half in range(2):
-            out_copy(chunk, half).start()
-
-    for n in range(15):
-        g_copy(n).wait_send()
-
-    @pl.loop(0, SLOTS)
-    def _(slot):
-        for n in range(15):
             d_copy(slot, n).wait_send()
-            m_copy(slot, n).wait_send()
         for hop in range(4):
             ahead_copy(slot, hop).wait_send()
         for hop in range(3):
@@ -308,24 +328,44 @@
         for n in range(8):
             partner_copy(slot, n).wait_send()
 
-    for chunk in range(4):
-        for half in range(2):
-            out_copy(chunk, half).wait()
+    @pl.loop(0, SLOTS - 1)
+    def _(slot):
+        for n in range(15):
+            m_copy(slot, n).wait_send()
+
+    for n in range(15):
+        m_copy(None, n).wait_send()
+
+
+def finish(acc_ref, m_last, inv_hi, inv_lo, out_ref):
+    first = pl.program_id(0) * 8
+    table_hi = inv_hi[96:128]
+    table_lo = inv_lo[96:128]
+    for u in range(8):
+        part = m_last[pl.ds(first + u, 32, stride=64), :]
+        high, low = split(part.T)
+        value = (
+            jnp.dot(high, table_hi, preferred_element_type=F32)
+            + jnp.dot(low, table_hi, preferred_element_type=F32)
+            + jnp.dot(high, table_lo, preferred_element_type=F32)
+        )
+        out_ref[0, u] = acc_ref[0, first + u] + value[:64]
+        out_ref[1, u] = acc_ref[1, first + u] + value[64:]
 
 
 def local(recorded, panels):
-    forward, inverse = lookup_tables()
+    tables = [jnp.asarray(table) for table in lookup_tables()]
     dma = pltpu.SemaphoreType.DMA
-    return pl.pallas_call(
+    whole = pl.BlockSpec(memory_space=pltpu.VMEM)
+    acc, last = pl.pallas_call(
         kernel,
-        out_shape=jax.ShapeDtypeStruct((128, 64, NT), F32),
+        out_shape=(pltpu.VMEM((128, 64, NT), F32), pltpu.VMEM((2048, 128), F32)),
         in_specs=[
             pl.BlockSpec(memory_space=pl.ANY),
             pl.BlockSpec(memory_space=pl.ANY),
-            pl.BlockSpec(memory_space=pltpu.VMEM),
-            pl.BlockSpec(memory_space=pltpu.VMEM),
+            whole, whole, whole, whole,
         ],
-        out_specs=pl.BlockSpec(memory_space=pl.ANY),
+        out_specs=(whole, whole),
         scratch_shapes=[
             pltpu.VMEM((128, 64, NT), F32),
             pltpu.VMEM((16, 64, NT), F32),
@@ -339,9 +379,8 @@
             pltpu.VMEM((2, 512, 512), BF16),
             pltpu.VMEM((2, 512, 512), BF16),
             pltpu.VMEM((SLOTS, 16, 128, 128), F32),
-            pltpu.VMEM((8192, 128), F32),
-            pltpu.VMEM((128, 64, NT), F32),
-            dma((4, 2)), dma, dma((4, 2)),
+            pltpu.VMEM((SLOTS - 1, 2048, 128), F32),
+            dma((4, 2)), dma,
             dma((15,)), dma((15,)),
             dma((SLOTS, 15)), dma((SLOTS, 15)),
             dma((SLOTS, 15)), dma((SLOTS, 15)),
@@ -350,10 +389,20 @@
             dma((SLOTS, 8)), dma((SLOTS, 8)),
         ],
         compiler_params=pltpu.CompilerParams(
-            collective_id=0, has_side_effects=True, vmem_limit_bytes=56 * 1024 * 1024
+            collective_id=0, has_side_effects=True, vmem_limit_bytes=50 * 1024 * 1024
         ),
         name="convolve",
-    )(recorded, panels, jnp.asarray(forward), jnp.asarray(inverse))
+    )(recorded, panels, *tables)
+    out = pl.pallas_call(
+        finish,
+        grid=(8,),
+        out_shape=jax.ShapeDtypeStruct((2, 64, 64, NT), F32),
+        in_specs=[whole, whole, whole, whole],
+        out_specs=pl.BlockSpec((2, 8, 64, NT), lambda g: (0, g, 0, 0)),
+        compiler_params=pltpu.CompilerParams(vmem_limit_bytes=16 * 1024 * 1024),
+        name="finish",
+    )(acc.reshape(2, 64, 64, NT), last, tables[2], tables[3])
+    return out.reshape(128, 64, NT)
 
 
 def solution(mesh):

time: 132 us -> 123 us (0.932)
  the two profiles are of different devices: /device:TPU:145 before, /device:TPU:6 now
where the time goes in v1:
time: 123 us; the launch traced here: 121 us
  Pallas kernels  121 us (98%)
    pallas_call x1, Pallas kernels, local(): pl.pallas_call(kernel, out_shape=(pltpu.VMEM((128, 64, NT), F32), pltpu.V...  115 us
    pallas_call x1, Pallas kernels, local(): pl.pallas_call(finish, grid=(8,), out_shape=jax.ShapeDtypeStruct((2, 64,...  5.57 us

profile of v1, /device:TPU:6, one launch (start us, length us, event | category | flops | bytes accessed | tf_op | source)
XLA Modules:
  0.0 120.9 jit_solution(8673652521097999329)
XLA Ops:
  0.0 0.0 copy-start
  0.0 0.0 copy-start.1
  0.0 115.3 %convolve.1 = (f32[128,64,128]{2,1,0:T(8,128)S(1)}, f32[2048,128]{1,0:T(8,128)S(1)}) custom-call(f32[128,64,128]{2,1,0:T(8,128)} %rec_hbm.1, f32[16,64,128]{2,1,0:T(8,128)} %pan_hbm.1, bf16[128,128]{1,0:T(8,128)(2,1)} %constant.8.clone.fwd_hi, bf16[128,128]{1,0:T(8,128)(2,1)} %constant.9.clone.fwd_lo, bf16[128,128]{1,0:T(8,128)(2,1)} %constant.10.clone.inv_hi, ...), custom_call_target="tpu_custom_call" | custom-call | tf_op jit(solution)/shard_map/convolve/pallas_call | solution.py:360
  115.4 0.0 copy-done
  115.4 0.0 copy-done.1
  115.4 5.6 %finish.1 = f32[2,64,64,128]{3,2,1,0:T(8,128)} custom-call(f32[2,64,64,128]{3,2,1,0:T(8,128)S(1)} %bitcast.2, f32[2048,128]{1,0:T(8,128)S(1)} %get-tuple-element.8.m_last, bf16[128,128]{1,0:T(8,128)(2,1)S(1)} %copy-done.1, bf16[128,128]{1,0:T(8,128)(2,1)S(1)} %copy-done), custom_call_target="tpu_custom_call" | custom-call | tf_op jit(solution)/shard_map/finish/pallas_call | solution.py:396
Async XLA Ops:
  0.0 115.4 %copy-start = (bf16[128,128]{1,0:T(8,128)(2,1)S(1)}, bf16[128,128]{1,0:T(8,128)(2,1)}, u32[]{:S(2)}) copy-start(bf16[128,128]{1,0:T(8,128)(2,1)} %constant.11.clone.inv_lo) | copy-start | bytes 98308
  0.0 115.4 %copy-start.1 = (bf16[128,128]{1,0:T(8,128)(2,1)S(1)}, bf16[128,128]{1,0:T(8,128)(2,1)}, u32[]{:S(2)}) copy-start(bf16[128,128]{1,0:T(8,128)(2,1)} %constant.10.clone.inv_hi) | copy-start | bytes 98308

commit v2 on v1

--- a/solution.py
+++ b/solution.py
@@ -11,6 +11,7 @@
 NT = 128
 NF = 64
 SLOTS = 4
+PITCH = 72
 MESH = pl.DeviceIdType.MESH
 F32 = jnp.float32
 BF16 = jnp.bfloat16
@@ -29,7 +30,9 @@
     inverse = forward * weight[:, None, None]
     forward = forward.reshape(2 * NF, NT)
     inverse = inverse.reshape(16, SLOTS, 2, NT).transpose(1, 0, 2, 3).reshape(2 * NF, NT)
-    return [np.asarray(part) for table in (forward, inverse) for part in split_table(table)]
+    tables = [np.asarray(part) for table in (forward, inverse) for part in split_table(table)]
+    tail_hi, tail_lo = (np.kron(np.eye(4), part[96:].astype(np.float32)).astype(BF16) for part in tables[2:])
+    return tables, (np.concatenate([tail_hi, tail_hi]), tail_lo)
 
 
 def split_table(table):
@@ -140,13 +143,13 @@
             ih = chunk * 16 + pair * 2
             rows = jnp.concatenate([x_buf[ih], x_buf[ih + 64], x_buf[ih + 1], x_buf[ih + 65]], axis=0)
             hat = forward(rows)
-            d_send[pl.ds(ih, 128, stride=64), :] = hat[:, :128]
-            d_send[pl.ds(ih + 1, 128, stride=64), :] = hat[:, 128:]
+            d_send[:, ih, :] = hat[:, :128]
+            d_send[:, ih + 1, :] = hat[:, 128:]
 
     def d_copy(slot, n):
         o, xhi = plane(PLANE[n])
         return pltpu.make_async_remote_copy(
-            src_ref=d_send.at[pl.ds(((xhi * 8 + o) * SLOTS + slot) * 128, 128)],
+            src_ref=d_send.at[pl.ds(((xhi * 8 + o) * SLOTS + slot) * 2, 2), pl.ds(0, 64)],
             dst_ref=d_recv.at[slot, own_q],
             send_sem=ds_sem.at[slot, n], recv_sem=dr_sem.at[slot, n],
             device_id=plane_id(PLANE[n]), device_id_type=MESH,
@@ -159,7 +162,7 @@
 
     @pl.loop(0, SLOTS)
     def _(slot):
-        d_recv[slot, own_q] = d_send[pl.ds((own_q * SLOTS + slot) * 128, 128), :]
+        d_recv[slot, own_q] = d_send[pl.ds((own_q * SLOTS + slot) * 2, 2), 0:64, :]
 
     for n in range(15):
         g_copy(n).wait_recv()
@@ -198,24 +201,32 @@
             device_id=partner_id, device_id_type=MESH,
         )
 
-    @pl.loop(0, SLOTS)
-    def _(slot):
+    def first(slot):
         ahead_copy(slot, 0).start()
         behind_copy(slot, 0).start()
         partner_copy(slot, 0).start()
 
-    for hop in range(4):
-        @pl.loop(0, SLOTS)
-        def _(slot):
-            ahead_copy(slot, hop).wait_recv()
-            if hop < 3:
-                ahead_copy(slot, hop + 1).start()
-            partner_copy(slot, hop + 1).start()
-            if hop < 3:
-                behind_copy(slot, hop).wait_recv()
-                if hop < 2:
-                    behind_copy(slot, hop + 1).start()
-                partner_copy(slot, hop + 5).start()
+    def pass_on(hop, slot):
+        ahead_copy(slot, hop).wait_recv()
+        if hop < 3:
+            ahead_copy(slot, hop + 1).start()
+        partner_copy(slot, hop + 1).start()
+        if hop < 3:
+            behind_copy(slot, hop).wait_recv()
+            if hop < 2:
+                behind_copy(slot, hop + 1).start()
+            partner_copy(slot, hop + 5).start()
+
+    first(0)
+    first(1)
+    pass_on(0, 0)
+    first(2)
+    pass_on(1, 0)
+    pass_on(0, 1)
+    first(3)
+    pass_on(2, 0)
+    pass_on(1, 1)
+    pass_on(0, 2)
 
     def m_copy(slot, n):
         o, xhi = plane(PLANE[n])
@@ -225,7 +236,7 @@
             dst = m_recv.at[slot]
         return pltpu.make_async_remote_copy(
             src_ref=m_send.at[slot, xhi * 8 + o],
-            dst_ref=dst.at[pl.ds(own_q * 128, 128)],
+            dst_ref=dst.at[pl.ds(own_q * 2, 2), pl.ds(0, 64)],
             send_sem=ms_sem.at[slot, n], recv_sem=mr_sem.at[slot, n],
             device_id=plane_id(PLANE[n]), device_id_type=MESH,
         )
@@ -252,9 +263,8 @@
         for xhi in range(2):
             for pair in range(4):
                 for c in range(2):
-                    rows = pl.ds(c * 64, 64)
                     top, bottom = halves(
-                        d_recv[slot, xhi * 8 + 2 * pair, rows, :], d_recv[slot, xhi * 8 + 2 * pair + 1, rows, :]
+                        d_recv[slot, xhi * 8 + 2 * pair, c], d_recv[slot, xhi * 8 + 2 * pair + 1, c]
                     )
                     for at, part in ((0, top), (64, bottom)):
                         high, low = split(part)
@@ -281,20 +291,32 @@
                         part = value[:, lanes * 128:(lanes + 1) * 128]
                         even, odd = halves(part[:64], part[64:])
                         o = tile * 4 + lanes * 2
-                        m_send[slot, xhi * 8 + o, c * 64:(c + 1) * 64, :] = even
-                        m_send[slot, xhi * 8 + o + 1, c * 64:(c + 1) * 64, :] = odd
+                        m_send[slot, xhi * 8 + o, c] = even
+                        m_send[slot, xhi * 8 + o + 1, c] = odd
 
     @pl.loop(0, SLOTS - 1)
     def _(slot):
+        pass_on(3, slot)
+        pass_on(2, slot + 1)
+
+        @pl.when(slot < 2)
+        def _():
+            pass_on(1, slot + 2)
+
+        @pl.when(slot < 1)
+        def _():
+            pass_on(0, slot + 3)
+
         predict(slot)
         for n in range(15):
             m_copy(slot, n).start()
-        m_recv[slot, pl.ds(own_q * 128, 128), :] = m_send[slot, own_q]
-
+        m_recv[slot, pl.ds(own_q * 2, 2), 0:64, :] = m_send[slot, own_q]
+
+    pass_on(3, SLOTS - 1)
     predict(SLOTS - 1)
     for n in range(15):
         m_copy(None, n).start()
-    m_last[pl.ds(own_q * 128, 128), :] = m_send[SLOTS - 1, own_q]
+    m_last[pl.ds(own_q * 2, 2), 0:64, :] = m_send[SLOTS - 1, own_q]
 
     @pl.loop(0, SLOTS - 1)
     def _(slot):
@@ -305,7 +327,7 @@
     def _(pair):
         for u in range(2):
             ih = pair * 2 + u
-            part = jnp.concatenate([m_recv[slot, pl.ds(ih, 32, stride=64), :] for slot in range(SLOTS - 1)], axis=0)
+            part = jnp.concatenate([m_recv[slot, :, ih, :] for slot in range(SLOTS - 1)], axis=0)
             high, low = split(part.T)
             value = dot(high, inv_hi[0:96]) + dot(low, inv_hi[0:96]) + dot(high, inv_lo[0:96])
             acc_ref[ih] = value[:64]
@@ -337,29 +359,41 @@
         m_copy(None, n).wait_send()
 
 
-def finish(acc_ref, m_last, inv_hi, inv_lo, out_ref):
-    first = pl.program_id(0) * 8
-    table_hi = inv_hi[96:128]
-    table_lo = inv_lo[96:128]
-    for u in range(8):
-        part = m_last[pl.ds(first + u, 32, stride=64), :]
-        high, low = split(part.T)
-        value = (
-            jnp.dot(high, table_hi, preferred_element_type=F32)
-            + jnp.dot(low, table_hi, preferred_element_type=F32)
-            + jnp.dot(high, table_lo, preferred_element_type=F32)
-        )
-        out_ref[0, u] = acc_ref[0, first + u] + value[:64]
-        out_ref[1, u] = acc_ref[1, first + u] + value[64:]
+def finish(acc_ref, m_last, tail_hi, tail_lo, out_hbm, o_buf, o_sem):
+    def out_copy(group, half):
+        rows = pl.ds(half * 64 + group * 4, 4)
+        return pltpu.make_async_copy(o_buf.at[rows], out_hbm.at[rows], o_sem.at[group, half])
+
+    @pl.loop(0, 8)
+    def _(pair):
+        for u in range(2):
+            group = pair * 2 + u
+            first = group * 4
+            part = jnp.concatenate([m_last[:, first + v, :] for v in range(4)], axis=0)
+            high, low = split(part.T)
+            value = jnp.dot(
+                jnp.concatenate([high, low], axis=1), tail_hi[...], preferred_element_type=F32
+            ) + jnp.dot(high, tail_lo[...], preferred_element_type=F32)
+            for v in range(4):
+                for half in range(2):
+                    at = half * 64 + first + v
+                    o_buf[at] = acc_ref[at] + value[half * 64:(half + 1) * 64, v * 128:(v + 1) * 128]
+            for half in range(2):
+                out_copy(group, half).start()
+
+    @pl.loop(0, 16)
+    def _(group):
+        for half in range(2):
+            out_copy(group, half).wait()
 
 
 def local(recorded, panels):
-    tables = [jnp.asarray(table) for table in lookup_tables()]
+    tables, tails = jax.tree.map(jnp.asarray, lookup_tables())
     dma = pltpu.SemaphoreType.DMA
     whole = pl.BlockSpec(memory_space=pltpu.VMEM)
     acc, last = pl.pallas_call(
         kernel,
-        out_shape=(pltpu.VMEM((128, 64, NT), F32), pltpu.VMEM((2048, 128), F32)),
+        out_shape=(pltpu.VMEM((128, 64, NT), F32), pltpu.VMEM((32, PITCH, 128), F32)),
         in_specs=[
             pl.BlockSpec(memory_space=pl.ANY),
             pl.BlockSpec(memory_space=pl.ANY),
@@ -372,14 +406,14 @@
             pltpu.VMEM((1024, 128), F32),
             pltpu.VMEM((16, 64, 128), F32),
             pltpu.VMEM((SLOTS, 16, 2, 2, 16, 512), F32),
-            pltpu.VMEM((8192, 128), F32),
-            pltpu.VMEM((SLOTS, 16, 128, 128), F32),
+            pltpu.VMEM((128, PITCH, 128), F32),
+            pltpu.VMEM((SLOTS, 16, 2, 64, 128), F32),
             pltpu.VMEM((2, 256, 512), BF16),
             pltpu.VMEM((2, 256, 512), BF16),
             pltpu.VMEM((2, 512, 512), BF16),
             pltpu.VMEM((2, 512, 512), BF16),
-            pltpu.VMEM((SLOTS, 16, 128, 128), F32),
-            pltpu.VMEM((SLOTS - 1, 2048, 128), F32),
+            pltpu.VMEM((SLOTS, 16, 2, 64, 128), F32),
+            pltpu.VMEM((SLOTS - 1, 32, PITCH, 128), F32),
             dma((4, 2)), dma,
             dma((15,)), dma((15,)),
             dma((SLOTS, 15)), dma((SLOTS, 15)),
@@ -389,20 +423,19 @@
             dma((SLOTS, 8)), dma((SLOTS, 8)),
         ],
         compiler_params=pltpu.CompilerParams(
-            collective_id=0, has_side_effects=True, vmem_limit_bytes=50 * 1024 * 1024
+            collective_id=0, has_side_effects=True, vmem_limit_bytes=52 * 1024 * 1024
         ),
         name="convolve",
     )(recorded, panels, *tables)
-    out = pl.pallas_call(
+    return pl.pallas_call(
         finish,
-        grid=(8,),
-        out_shape=jax.ShapeDtypeStruct((2, 64, 64, NT), F32),
+        out_shape=jax.ShapeDtypeStruct((128, 64, NT), F32),
         in_specs=[whole, whole, whole, whole],
-        out_specs=pl.BlockSpec((2, 8, 64, NT), lambda g: (0, g, 0, 0)),
+        out_specs=pl.BlockSpec(memory_space=pl.ANY),
+        scratch_shapes=[pltpu.VMEM((128, 64, NT), F32), dma((16, 2))],
         compiler_params=pltpu.CompilerParams(vmem_limit_bytes=16 * 1024 * 1024),
         name="finish",
-    )(acc.reshape(2, 64, 64, NT), last, tables[2], tables[3])
-    return out.reshape(128, 64, NT)
+    )(acc, last, *tails)
 
 
 def solution(mesh):

time: 123 us -> 118 us (0.959); the launches traced: 121 us -> 118 us
  Pallas kernels: 121 us -> 118 us
    pallas_call x1, Pallas kernels: 5.57 us -> 3.86 us  [local(): pl.pallas_call(finish, out_shape=jax.ShapeDtypeStruct((128, 64, NT), F32)...]
where the time goes in v2:
time: 118 us
  Pallas kernels  118 us (100%)
    pallas_call x1, Pallas kernels, local(): pl.pallas_call(kernel, out_shape=(pltpu.VMEM((128, 64, NT), F32), pltpu.V...  114 us
    pallas_call x1, Pallas kernels, local(): pl.pallas_call(finish, out_shape=jax.ShapeDtypeStruct((128, 64, NT), F32)...  3.86 us

profile of v2, /device:TPU:6, one launch (start us, length us, event | category | flops | bytes accessed | tf_op | source)
XLA Modules:
  0.0 118.1 jit_solution(7748819291752079043)
XLA Ops:
  0.0 0.0 copy-start.1
  0.0 0.0 copy-start
  0.0 114.2 %convolve.1 = (f32[128,64,128]{2,1,0:T(8,128)S(1)}, f32[32,72,128]{2,1,0:T(8,128)S(1)}) custom-call(f32[128,64,128]{2,1,0:T(8,128)} %rec_hbm.1, f32[16,64,128]{2,1,0:T(8,128)} %pan_hbm.1, bf16[128,128]{1,0:T(8,128)(2,1)} %constant.12.clone.fwd_hi, bf16[128,128]{1,0:T(8,128)(2,1)} %constant.13.clone.fwd_lo, bf16[128,128]{1,0:T(8,128)(2,1)} %constant.14.clone.inv_hi, ...), custom_call_target="tpu_custom_call" | custom-call | tf_op jit(solution)/shard_map/convolve/pallas_call | solution.py:394
  114.2 0.0 copy-done.1
  114.2 0.0 copy-done
  114.2 3.9 %finish.1 = f32[128,64,128]{2,1,0:T(8,128)} custom-call(f32[128,64,128]{2,1,0:T(8,128)S(1)} %get-tuple-element.7.acc_ref, f32[32,72,128]{2,1,0:T(8,128)S(1)} %get-tuple-element.8.m_last, bf16[256,512]{1,0:T(8,128)(2,1)S(1)} %copy-done, bf16[128,512]{1,0:T(8,128)(2,1)S(1)} %copy-done.1), custom_call_target="tpu_custom_call" | custom-call | tf_op jit(solution)/shard_map/finish/pallas_call | solution.py:430
Async XLA Ops:
  0.0 114.2 %copy-start.1 = (bf16[128,512]{1,0:T(8,128)(2,1)S(1)}, bf16[128,512]{1,0:T(8,128)(2,1)}, u32[]{:S(2)}) copy-start(bf16[128,512]{1,0:T(8,128)(2,1)} %constant.17.clone.tail_lo) | copy-start | bytes 393220
  0.0 114.2 %copy-start = (bf16[256,512]{1,0:T(8,128)(2,1)S(1)}, bf16[256,512]{1,0:T(8,128)(2,1)}, u32[]{:S(2)}) copy-start(bf16[256,512]{1,0:T(8,128)(2,1)} %constant.16.clone.tail_hi) | copy-start | bytes 786436

commit v3 on v2

--- a/solution.py
+++ b/solution.py
@@ -28,10 +28,12 @@
     forward = np.stack([np.cos(angle), -np.sin(angle)], axis=1)
     weight = np.where(np.arange(NF) == 0, 1.0, 2.0) / NT
     inverse = forward * weight[:, None, None]
-    forward = forward.reshape(2 * NF, NT)
-    inverse = inverse.reshape(16, SLOTS, 2, NT).transpose(1, 0, 2, 3).reshape(2 * NF, NT)
-    tables = [np.asarray(part) for table in (forward, inverse) for part in split_table(table)]
-    tail_hi, tail_lo = (np.kron(np.eye(4), part[96:].astype(np.float32)).astype(BF16) for part in tables[2:])
+    by_owner = forward.reshape(2 * NF, NT)
+    forward, inverse = (
+        table.reshape(16, SLOTS, 2, NT).transpose(1, 0, 2, 3).reshape(2 * NF, NT) for table in (forward, inverse)
+    )
+    tables = np.stack([part for table in (by_owner, forward, inverse) for part in split_table(table)])
+    tail_hi, tail_lo = (np.kron(np.eye(4), part[96:].astype(np.float32)).astype(BF16) for part in tables[4:])
     return tables, (np.concatenate([tail_hi, tail_hi]), tail_lo)
 
 
@@ -54,9 +56,9 @@
 
 
 def kernel(
-    rec_hbm, pan_hbm, fwd_hi, fwd_lo, inv_hi, inv_lo, acc_ref, m_last,
-    x_buf, p_buf, g_send, g_recv, g_all, d_send, d_recv, d_hi, d_lo, g_hi, g_lo, m_send, m_recv,
-    x_sem, p_sem, gs_sem, gr_sem, ds_sem, dr_sem, ms_sem, mr_sem,
+    rec_hbm, pan_hbm, table_hbm, acc_ref, m_last,
+    tables, x_buf, p_buf, g_send, g_recv, g_all, d_send, d_recv, d_hi, d_lo, g_hi, g_lo, m_send, m_recv,
+    t_sem, x_sem, p_sem, gs_sem, gr_sem, ds_sem, dr_sem, ms_sem, mr_sem,
     fs_sem, fr_sem, bs_sem, br_sem, cs_sem, cr_sem,
 ):
     own_o = lax.axis_index("freq")
@@ -88,6 +90,8 @@
 
     pan_copy = pltpu.make_async_copy(pan_hbm, p_buf, p_sem)
     pan_copy.start()
+    table_copy = pltpu.make_async_copy(table_hbm, tables, t_sem)
+    table_copy.start()
 
     def rec_copy(chunk, half):
         rows = pl.ds(half * 64 + chunk * 16, 16)
@@ -104,18 +108,20 @@
 
     nt = (((1,), (1,)), ((), ()))
 
-    def forward(rows):
+    def forward(table, freqs, rows):
         high, low = split(rows)
+        fwd_hi, fwd_lo = tables[table, freqs, :], tables[table + 1, freqs, :]
         return (
-            lax.dot_general(fwd_hi[...], high, nt, preferred_element_type=F32)
-            + lax.dot_general(fwd_hi[...], low, nt, preferred_element_type=F32)
-            + lax.dot_general(fwd_lo[...], high, nt, preferred_element_type=F32)
+            lax.dot_general(fwd_hi, high, nt, preferred_element_type=F32)
+            + lax.dot_general(fwd_hi, low, nt, preferred_element_type=F32)
+            + lax.dot_general(fwd_lo, high, nt, preferred_element_type=F32)
         )
 
     pan_copy.wait()
+    table_copy.wait()
     for kp in range(0, 8, 2):
         rows = jnp.concatenate([p_buf[kp], p_buf[kp + 8], p_buf[kp + 1], p_buf[kp + 9]], axis=0)
-        hat = forward(rows)
+        hat = forward(0, slice(0, 128), rows)
         g_send[pl.ds(kp, 128, stride=8), :] = hat[:, :128]
         g_send[pl.ds(kp + 1, 128, stride=8), :] = hat[:, 128:]
 
@@ -134,35 +140,45 @@
         g_copy(n).start()
     g_recv[own_q] = g_send[pl.ds(own_q * 64, 64), :]
 
+    def d_copy(slot, n):
+        o, xhi = plane(PLANE[n])
+        return pltpu.make_async_remote_copy(
+            src_ref=d_send.at[pl.ds(slot * 32 + (xhi * 8 + o) * 2, 2), pl.ds(0, 64)],
+            dst_ref=d_recv.at[slot, own_q],
+            send_sem=ds_sem.at[slot, n], recv_sem=dr_sem.at[slot, n],
+            device_id=plane_id(PLANE[n]), device_id_type=MESH,
+        )
+
+    def spectra(start, count, ih):
+        rows = jnp.concatenate([x_buf[ih], x_buf[ih + 64], x_buf[ih + 1], x_buf[ih + 65]], axis=0)
+        freqs = slice(start, start + count)
+        hat = forward(2, freqs, rows)
+        d_send[freqs, ih, :] = hat[:, :128]
+        d_send[freqs, ih + 1, :] = hat[:, 128:]
+
+    def d_start(slot):
+        for n in range(15):
+            d_copy(slot, n).start()
+        d_recv[slot, own_q] = d_send[pl.ds(slot * 32 + own_q * 2, 2), 0:64, :]
+
     for chunk in range(4):
         for half in range(2):
             rec_copy(chunk, half).wait()
 
-        @pl.loop(0, 8)
-        def _(pair):
-            ih = chunk * 16 + pair * 2
-            rows = jnp.concatenate([x_buf[ih], x_buf[ih + 64], x_buf[ih + 1], x_buf[ih + 65]], axis=0)
-            hat = forward(rows)
-            d_send[:, ih, :] = hat[:, :128]
-            d_send[:, ih + 1, :] = hat[:, 128:]
-
-    def d_copy(slot, n):
-        o, xhi = plane(PLANE[n])
-        return pltpu.make_async_remote_copy(
-            src_ref=d_send.at[pl.ds(((xhi * 8 + o) * SLOTS + slot) * 2, 2), pl.ds(0, 64)],
-            dst_ref=d_recv.at[slot, own_q],
-            send_sem=ds_sem.at[slot, n], recv_sem=dr_sem.at[slot, n],
-            device_id=plane_id(PLANE[n]), device_id_type=MESH,
-        )
-
-    @pl.loop(0, SLOTS)
+        @pl.loop(0, 4)
+        def _(quad):
+            for u in range(2):
+                spectra(0, 32, chunk * 16 + quad * 4 + u * 2)
+
+    d_start(0)
+
+    @pl.loop(0, 32)
+    def _(pair):
+        spectra(32, 96, pair * 2)
+
+    @pl.loop(1, SLOTS)
     def _(slot):
-        for n in range(15):
-            d_copy(slot, n).start()
-
-    @pl.loop(0, SLOTS)
-    def _(slot):
-        d_recv[slot, own_q] = d_send[pl.ds((own_q * SLOTS + slot) * 2, 2), 0:64, :]
+        d_start(slot)
 
     for n in range(15):
         g_copy(n).wait_recv()
@@ -318,20 +334,37 @@
         m_copy(None, n).start()
     m_last[pl.ds(own_q * 2, 2), 0:64, :] = m_send[SLOTS - 1, own_q]
 
-    @pl.loop(0, SLOTS - 1)
-    def _(slot):
+    def arrive(slot):
         for n in range(15):
             m_copy(slot, n).wait_recv()
+
+    def back(first, slots, ih):
+        part = jnp.concatenate([m_recv[slot, :, ih, :] for slot in range(first, first + slots)], axis=0)
+        high, low = split(part.T)
+        freqs = slice(first * 32, (first + slots) * 32)
+        inv_hi, inv_lo = tables[4, freqs, :], tables[5, freqs, :]
+        return dot(high, inv_hi) + dot(low, inv_hi) + dot(high, inv_lo)
+
+    arrive(0)
+    arrive(1)
 
     @pl.loop(0, 32)
     def _(pair):
         for u in range(2):
             ih = pair * 2 + u
-            part = jnp.concatenate([m_recv[slot, :, ih, :] for slot in range(SLOTS - 1)], axis=0)
-            high, low = split(part.T)
-            value = dot(high, inv_hi[0:96]) + dot(low, inv_hi[0:96]) + dot(high, inv_lo[0:96])
+            value = back(0, 2, ih)
             acc_ref[ih] = value[:64]
             acc_ref[ih + 64] = value[64:]
+
+    arrive(2)
+
+    @pl.loop(0, 32)
+    def _(pair):
+        for u in range(2):
+            ih = pair * 2 + u
+            value = back(2, 1, ih)
+            acc_ref[ih] += value[:64]
+            acc_ref[ih + 64] += value[64:]
 
     for n in range(15):
         m_copy(None, n).wait_recv()
@@ -397,10 +430,11 @@
         in_specs=[
             pl.BlockSpec(memory_space=pl.ANY),
             pl.BlockSpec(memory_space=pl.ANY),
-            whole, whole, whole, whole,
+            pl.BlockSpec(memory_space=pl.ANY),
         ],
         out_specs=(whole, whole),
         scratch_shapes=[
+            pltpu.VMEM((6, 128, NT), BF16),
             pltpu.VMEM((128, 64, NT), F32),
             pltpu.VMEM((16, 64, NT), F32),
             pltpu.VMEM((1024, 128), F32),
@@ -414,7 +448,7 @@
             pltpu.VMEM((2, 512, 512), BF16),
             pltpu.VMEM((SLOTS, 16, 2, 64, 128), F32),
             pltpu.VMEM((SLOTS - 1, 32, PITCH, 128), F32),
-            dma((4, 2)), dma,
+            dma, dma((4, 2)), dma,
             dma((15,)), dma((15,)),
             dma((SLOTS, 15)), dma((SLOTS, 15)),
             dma((SLOTS, 15)), dma((SLOTS, 15)),
@@ -426,7 +460,7 @@
             collective_id=0, has_side_effects=True, vmem_limit_bytes=52 * 1024 * 1024
         ),
         name="convolve",
-    )(recorded, panels, *tables)
+    )(recorded, panels, tables)
     return pl.pallas_call(
         finish,
         out_shape=jax.ShapeDtypeStruct((128, 64, NT), F32),

time: 118 us -> 115 us (0.975); the launches traced: 118 us -> 113 us
  Pallas kernels: 118 us -> 113 us
    pallas_call x1, Pallas kernels: 114 us -> 109 us  [local(): pl.pallas_call(kernel, out_shape=(pltpu.VMEM((128, 64, NT), F32), pltpu.V...]
where the time goes in v3:
time: 115 us; the launch traced here: 113 us
  Pallas kernels  113 us (98%)
    pallas_call x1, Pallas kernels, local(): pl.pallas_call(kernel, out_shape=(pltpu.VMEM((128, 64, NT), F32), pltpu.V...  109 us
    pallas_call x1, Pallas kernels, local(): pl.pallas_call(finish, out_shape=jax.ShapeDtypeStruct((128, 64, NT), F32)...  3.86 us

profile of v3, /device:TPU:6, one launch (start us, length us, event | category | flops | bytes accessed | tf_op | source)
XLA Modules:
  0.0 113.0 jit_solution(12194176448912279551)
XLA Ops:
  0.0 0.0 copy-start.1
  0.0 0.0 copy-start
  0.0 109.1 %convolve.1 = (f32[128,64,128]{2,1,0:T(8,128)S(1)}, f32[32,72,128]{2,1,0:T(8,128)S(1)}) custom-call(f32[128,64,128]{2,1,0:T(8,128)} %rec_hbm.1, f32[16,64,128]{2,1,0:T(8,128)} %pan_hbm.1, bf16[6,128,128]{2,1,0:T(8,128)(2,1)} %constant.6.clone.table_hbm), custom_call_target="tpu_custom_call" | custom-call | tf_op jit(solution)/shard_map/convolve/pallas_call | solution.py:427
  109.1 0.0 copy-done.1
  109.1 0.0 copy-done
  109.1 3.9 %finish.1 = f32[128,64,128]{2,1,0:T(8,128)} custom-call(f32[128,64,128]{2,1,0:T(8,128)S(1)} %get-tuple-element.7.acc_ref, f32[32,72,128]{2,1,0:T(8,128)S(1)} %get-tuple-element.8.m_last, bf16[256,512]{1,0:T(8,128)(2,1)S(1)} %copy-done, bf16[128,512]{1,0:T(8,128)(2,1)S(1)} %copy-done.1), custom_call_target="tpu_custom_call" | custom-call | tf_op jit(solution)/shard_map/finish/pallas_call | solution.py:464
Async XLA Ops:
  0.0 109.1 %copy-start.1 = (bf16[128,512]{1,0:T(8,128)(2,1)S(1)}, bf16[128,512]{1,0:T(8,128)(2,1)}, u32[]{:S(2)}) copy-start(bf16[128,512]{1,0:T(8,128)(2,1)} %constant.8.clone.tail_lo) | copy-start | bytes 393220
  0.0 109.1 %copy-start = (bf16[256,512]{1,0:T(8,128)(2,1)S(1)}, bf16[256,512]{1,0:T(8,128)(2,1)}, u32[]{:S(2)}) copy-start(bf16[256,512]{1,0:T(8,128)(2,1)} %constant.7.clone.tail_hi) | copy-start | bytes 786436

commit v4 on v3

--- a/solution.py
+++ b/solution.py
@@ -12,6 +12,7 @@
 NF = 64
 SLOTS = 4
 PITCH = 72
+GROUPS = 4
 MESH = pl.DeviceIdType.MESH
 F32 = jnp.float32
 BF16 = jnp.bfloat16
@@ -122,15 +123,15 @@
     for kp in range(0, 8, 2):
         rows = jnp.concatenate([p_buf[kp], p_buf[kp + 8], p_buf[kp + 1], p_buf[kp + 9]], axis=0)
         hat = forward(0, slice(0, 128), rows)
-        g_send[pl.ds(kp, 128, stride=8), :] = hat[:, :128]
-        g_send[pl.ds(kp + 1, 128, stride=8), :] = hat[:, 128:]
+        g_send[kp] = hat[:, :128]
+        g_send[kp + 1] = hat[:, 128:]
 
     pl.semaphore_wait(barrier, len(others))
 
     def g_copy(n):
         o, xhi = plane(PLANE[n])
         return pltpu.make_async_remote_copy(
-            src_ref=g_send.at[pl.ds((xhi * 8 + o) * 64, 64)],
+            src_ref=g_send.at[:, pl.ds((xhi * 8 + o) * 8, 8)],
             dst_ref=g_recv.at[own_q],
             send_sem=gs_sem.at[n], recv_sem=gr_sem.at[n],
             device_id=plane_id(PLANE[n]), device_id_type=MESH,
@@ -138,7 +139,7 @@
 
     for n in range(15):
         g_copy(n).start()
-    g_recv[own_q] = g_send[pl.ds(own_q * 64, 64), :]
+    g_recv[own_q] = g_send[:, pl.ds(own_q * 8, 8), :]
 
     def d_copy(slot, n):
         o, xhi = plane(PLANE[n])
@@ -186,10 +187,12 @@
     @pl.loop(0, SLOTS)
     def _(slot):
         for c in range(2):
-            rows = pl.ds((slot * 2 + c) * 8, 8)
+            row = slot * 2 + c
             for xhi in range(2):
                 for pair in range(4):
-                    low, high = halves(g_recv[xhi * 8 + 2 * pair, rows, :], g_recv[xhi * 8 + 2 * pair + 1, rows, :])
+                    low, high = halves(
+                        g_recv[xhi * 8 + 2 * pair, :, row, :], g_recv[xhi * 8 + 2 * pair + 1, :, row, :]
+                    )
                     g_all[slot, zc, c, xhi, 0:8, pair * 128:(pair + 1) * 128] = low
                     g_all[slot, zc, c, xhi, 8:16, pair * 128:(pair + 1) * 128] = high
 
@@ -397,20 +400,25 @@
         rows = pl.ds(half * 64 + group * 4, 4)
         return pltpu.make_async_copy(o_buf.at[rows], out_hbm.at[rows], o_sem.at[group, half])
 
-    @pl.loop(0, 8)
-    def _(pair):
-        for u in range(2):
-            group = pair * 2 + u
-            first = group * 4
-            part = jnp.concatenate([m_last[:, first + v, :] for v in range(4)], axis=0)
-            high, low = split(part.T)
-            value = jnp.dot(
-                jnp.concatenate([high, low], axis=1), tail_hi[...], preferred_element_type=F32
-            ) + jnp.dot(high, tail_lo[...], preferred_element_type=F32)
+    @pl.loop(0, 16 // GROUPS)
+    def _(step):
+        parts = []
+        for u in range(GROUPS):
+            first = (step * GROUPS + u) * 4
+            part = jnp.concatenate([m_last[pl.ds(first + v, 32, stride=PITCH), :] for v in range(4)], axis=0)
+            parts.append(split(part.T))
+        both = jnp.concatenate([jnp.concatenate(part, axis=1) for part in parts], axis=0)
+        highs = jnp.concatenate([high for high, _ in parts], axis=0)
+        value = jnp.dot(both, tail_hi[...], preferred_element_type=F32) + jnp.dot(
+            highs, tail_lo[...], preferred_element_type=F32
+        )
+        for u in range(GROUPS):
+            group = step * GROUPS + u
             for v in range(4):
                 for half in range(2):
-                    at = half * 64 + first + v
-                    o_buf[at] = acc_ref[at] + value[half * 64:(half + 1) * 64, v * 128:(v + 1) * 128]
+                    at = half * 64 + group * 4 + v
+                    rows = slice(u * 128 + half * 64, u * 128 + (half + 1) * 64)
+                    o_buf[at] = acc_ref[at] + value[rows, v * 128:(v + 1) * 128]
             for half in range(2):
                 out_copy(group, half).start()
 
@@ -437,8 +445,8 @@
             pltpu.VMEM((6, 128, NT), BF16),
             pltpu.VMEM((128, 64, NT), F32),
             pltpu.VMEM((16, 64, NT), F32),
-            pltpu.VMEM((1024, 128), F32),
-            pltpu.VMEM((16, 64, 128), F32),
+            pltpu.VMEM((8, 128, 128), F32),
+            pltpu.VMEM((16, 8, 8, 128), F32),
             pltpu.VMEM((SLOTS, 16, 2, 2, 16, 512), F32),
             pltpu.VMEM((128, PITCH, 128), F32),
             pltpu.VMEM((SLOTS, 16, 2, 64, 128), F32),
@@ -469,7 +477,7 @@
         scratch_shapes=[pltpu.VMEM((128, 64, NT), F32), dma((16, 2))],
         compiler_params=pltpu.CompilerParams(vmem_limit_bytes=16 * 1024 * 1024),
         name="finish",
-    )(acc, last, *tails)
+    )(acc, last.reshape(32 * PITCH, 128), *tails)
 
 
 def solution(mesh):

time: 115 us -> 114 us (level)
  no operation moved by 1% of the time
where the time goes in v4:
time: 114 us; the launch traced here: 112 us
  Pallas kernels  112 us (98%)
    pallas_call x1, Pallas kernels, local(): pl.pallas_call(kernel, out_shape=(pltpu.VMEM((128, 64, NT), F32), pltpu.V...  109 us
    pallas_call x1, Pallas kernels, local(): pl.pallas_call(finish, out_shape=jax.ShapeDtypeStruct((128, 64, NT), F32)...  3.09 us

profile of v4, /device:TPU:6, one launch (start us, length us, event | category | flops | bytes accessed | tf_op | source)
XLA Modules:
  0.0 112.2 jit_solution(6468172475185264562)
XLA Ops:
  0.0 0.0 copy-start.1
  0.0 0.0 copy-start
  0.0 109.1 %convolve.1 = (f32[128,64,128]{2,1,0:T(8,128)S(1)}, f32[32,72,128]{2,1,0:T(8,128)S(1)}) custom-call(f32[128,64,128]{2,1,0:T(8,128)} %rec_hbm.1, f32[16,64,128]{2,1,0:T(8,128)} %pan_hbm.1, bf16[6,128,128]{2,1,0:T(8,128)(2,1)} %constant.6.clone.table_hbm), custom_call_target="tpu_custom_call" | custom-call | tf_op jit(solution)/shard_map/convolve/pallas_call | solution.py:435
  109.1 0.0 copy-done.1
  109.1 0.0 copy-done
  109.1 3.1 %finish.1 = f32[128,64,128]{2,1,0:T(8,128)} custom-call(f32[128,64,128]{2,1,0:T(8,128)S(1)} %get-tuple-element.7.acc_ref, f32[2304,128]{1,0:T(8,128)S(1)} %bitcast.1, bf16[256,512]{1,0:T(8,128)(2,1)S(1)} %copy-done, bf16[128,512]{1,0:T(8,128)(2,1)S(1)} %copy-done.1), custom_call_target="tpu_custom_call" | custom-call | tf_op jit(solution)/shard_map/finish/pallas_call | solution.py:472
Async XLA Ops:
  0.0 109.1 %copy-start.1 = (bf16[128,512]{1,0:T(8,128)(2,1)S(1)}, bf16[128,512]{1,0:T(8,128)(2,1)}, u32[]{:S(2)}) copy-start(bf16[128,512]{1,0:T(8,128)(2,1)} %constant.8.clone.tail_lo) | copy-start | bytes 393220
  0.0 109.1 %copy-start = (bf16[256,512]{1,0:T(8,128)(2,1)S(1)}, bf16[256,512]{1,0:T(8,128)(2,1)}, u32[]{:S(2)}) copy-start(bf16[256,512]{1,0:T(8,128)(2,1)} %constant.7.clone.tail_hi) | copy-start | bytes 786436

commit v5 on v4

--- a/solution.py
+++ b/solution.py
@@ -12,7 +12,7 @@
 NF = 64
 SLOTS = 4
 PITCH = 72
-GROUPS = 4
+GROUPS = 8
 MESH = pl.DeviceIdType.MESH
 F32 = jnp.float32
 BF16 = jnp.bfloat16

time: 114 us -> 114 us (level)
  no operation moved by 1% of the time
where the time goes in v5:
time: 114 us; the launch traced here: 112 us
  Pallas kernels  112 us (98%)
    pallas_call x1, Pallas kernels, local(): pl.pallas_call(kernel, out_shape=(pltpu.VMEM((128, 64, NT), F32), pltpu.V...  109 us
    pallas_call x1, Pallas kernels, local(): pl.pallas_call(finish, out_shape=jax.ShapeDtypeStruct((128, 64, NT), F32)...  2.87 us

profile of v5, /device:TPU:6, one launch (start us, length us, event | category | flops | bytes accessed | tf_op | source)
XLA Modules:
  0.0 112.0 jit_solution(13834804724160855732)
XLA Ops:
  0.0 0.0 copy-start.1
  0.0 0.0 copy-start
  0.0 109.1 %convolve.1 = (f32[128,64,128]{2,1,0:T(8,128)S(1)}, f32[32,72,128]{2,1,0:T(8,128)S(1)}) custom-call(f32[128,64,128]{2,1,0:T(8,128)} %rec_hbm.1, f32[16,64,128]{2,1,0:T(8,128)} %pan_hbm.1, bf16[6,128,128]{2,1,0:T(8,128)(2,1)} %constant.6.clone.table_hbm), custom_call_target="tpu_custom_call" | custom-call | tf_op jit(solution)/shard_map/convolve/pallas_call | solution.py:435
  109.1 0.0 copy-done.1
  109.1 0.0 copy-done
  109.1 2.9 %finish.1 = f32[128,64,128]{2,1,0:T(8,128)} custom-call(f32[128,64,128]{2,1,0:T(8,128)S(1)} %get-tuple-element.7.acc_ref, f32[2304,128]{1,0:T(8,128)S(1)} %bitcast.1, bf16[256,512]{1,0:T(8,128)(2,1)S(1)} %copy-done, bf16[128,512]{1,0:T(8,128)(2,1)S(1)} %copy-done.1), custom_call_target="tpu_custom_call" | custom-call | tf_op jit(solution)/shard_map/finish/pallas_call | solution.py:472
Async XLA Ops:
  0.0 109.1 %copy-start.1 = (bf16[128,512]{1,0:T(8,128)(2,1)S(1)}, bf16[128,512]{1,0:T(8,128)(2,1)}, u32[]{:S(2)}) copy-start(bf16[128,512]{1,0:T(8,128)(2,1)} %constant.8.clone.tail_lo) | copy-start | bytes 393220
  0.0 109.1 %copy-start = (bf16[256,512]{1,0:T(8,128)(2,1)S(1)}, bf16[256,512]{1,0:T(8,128)(2,1)}, u32[]{:S(2)}) copy-start(bf16[256,512]{1,0:T(8,128)(2,1)} %constant.7.clone.tail_hi) | copy-start | bytes 786436
